TPU v7x, 256 devices: a 2x2x32 block of a 4x8x32 slice. The times are simulated.
256 devices in a mesh: group: 4 (over x, y), lat: 64 (over z, core).
Axes of the slice: x: 2, y: 2, z: 32, core: 2. Of those that a mesh axis runs over, the one named last changes fastest.
The devices are a block of a 4x8x32 slice.
Arguments:
- grid_values: bfloat16 [1792, 1440, 256], P(('group', 'lat')), parts along dimension 0, may hold values from -630 to 630
- lat_counts: int32 [64], replicated, may hold values from 1 to 7, 384 in all
- owner_wavenumber: int32 [384], replicated, may hold values from 0 to 383, each once
- legendre: bfloat16 [384, 384, 384], P('lat'), may hold values from -0.3125 to 0.3125
- quad_weight: float32 [384], replicated, may hold values from 0.3 to 3
- spectral_gain: float32 [384, 256], replicated, may hold values from 0.3 to 3
- channel_mix: bfloat16 [256, 256], replicated, may hold values from -0.375 to 0.375
Outputs:
- grid_output: bfloat16 [1792, 1440, 256], P(('group', 'lat')), parts along dimension 0
There are 4 independent parts, one for each index of `group`. A program takes and returns all parts, laid end to end along the dimension named above; an argument that names none is the same for every part. Nothing has to cross between parts.
Inputs may be any that keep to these rules, and one draw needn't show every extreme that they name: `lat_counts`: some device has all 7 slots live. `owner_wavenumber`: each wavenumber appears once; device i of lat owns wavenumber slots i * 6 to (i + 1) * 6 - 1.
All inputs are finite; a program needn't handle non-finite values.
Results may differ from a plain program's by a relative error of at most 0.0095.
Values may be sent and summed in bfloat16 or wider, within the bound.
A program may use at most 64 MiB of HBM per device.

v0:
```python
import math

import jax
import jax.numpy as jnp
from jax import lax
from jax.sharding import PartitionSpec as P


def from_everyone(shard, axis):
    copies = jnp.broadcast_to(shard, (lax.axis_size(axis), *shard.shape))
    return lax.all_to_all(copies, axis, split_axis=0, concat_axis=0, tiled=True)


def over_copies(shard, axis):
    everything = from_everyone(shard, axis)
    return jnp.sum(everything, axis=0)


def packed_total(arrays, axis):
    flat, at, gathered = (jnp.concatenate([a.reshape(-1) for a in arrays]), 0, [])
    subtotal = over_copies(flat, axis)
    for a in arrays:
        gathered.append(subtotal[at : at + a.size].reshape(a.shape))
        at += a.size
    return tuple(gathered)


def live_slots(lat_counts, slot_count, live_total):
    devices = lat_counts.shape[0]
    starts = jnp.cumsum(lat_counts) - lat_counts
    device_ids = jnp.arange(devices, dtype=jnp.int32)
    slot_ids = jnp.arange(devices * slot_count, dtype=jnp.int32)
    holder = slot_ids // slot_count
    within = slot_ids - holder * slot_count
    holder_hot = holder[:, None] == device_ids[None, :]
    holder_count = jnp.sum(jnp.where(holder_hot, lat_counts[None, :], 0), axis=1)
    holder_start = jnp.sum(jnp.where(holder_hot, starts[None, :], 0), axis=1)
    slot_valid = within < holder_count
    slot_live = jnp.where(slot_valid, holder_start + within, 0)
    live_ids = jnp.arange(live_total, dtype=jnp.int32)
    reached = (starts[None, :] <= live_ids[:, None]).astype(jnp.int32)
    source = jnp.sum(reached, axis=1) - 1
    source_hot = source[:, None] == device_ids[None, :]
    source_start = jnp.sum(jnp.where(source_hot, starts[None, :], 0), axis=1)
    live_slot = source * slot_count + live_ids - source_start
    return (slot_valid, slot_live, live_slot)


def wave_angles(wave_list, longitudes):
    points = jnp.arange(longitudes, dtype=jnp.int32)
    phase = wave_list[:, None] * points[None, :] % longitudes
    return phase.astype(jnp.float32) * (2.0 * math.pi / longitudes)


def forward_table(wave_list, longitudes):
    angle = wave_angles(wave_list, longitudes)
    factor = 1.0 / math.sqrt(longitudes)
    return jnp.stack([jnp.cos(angle) * factor, -jnp.sin(angle) * factor], axis=1).astype(
        jnp.bfloat16
    )


def inverse_table(wave_list, longitudes):
    angle = wave_angles(wave_list, longitudes)
    factor = 1.0 / math.sqrt(longitudes)
    doubled = jnp.where(wave_list > 0, 2.0, 1.0).astype(jnp.float32)[:, None] * factor
    return jnp.stack([jnp.cos(angle) * doubled, -jnp.sin(angle) * doubled], axis=1).astype(
        jnp.bfloat16
    )


def body(
    grid_values, lat_counts, owner_wavenumber, legendre, quad_weight, spectral_gain, channel_mix
):
    slot_count, longitudes, channels = grid_values.shape
    my_index = lax.axis_index("lat")
    wave_count = owner_wavenumber.shape[0]
    wave_share, live_total, degrees = legendre.shape
    slot_valid, slot_live, live_slot = live_slots(lat_counts, slot_count, live_total)
    local_valid = lax.dynamic_slice_in_dim(slot_valid, my_index * slot_count, slot_count)
    row_weight = local_valid.astype(jnp.float32)[:, None, None]
    widened = grid_values.astype(jnp.float32) * row_weight
    totals = packed_total(
        (jnp.sum(widened, axis=(0, 1)), jnp.sum(widened * widened, axis=(0, 1))), "lat"
    )
    points = live_total * longitudes
    channel_mean = totals[0] / points
    variance = totals[1] / points - channel_mean * channel_mean
    normed = (
        (grid_values.astype(jnp.float32) - channel_mean) * lax.rsqrt(variance + 1e-05) * row_weight
    ).astype(jnp.bfloat16)
    forward_flat = forward_table(owner_wavenumber, longitudes).reshape(2 * wave_count, longitudes)
    spectra = jnp.einsum("skc,qk->sqc", normed, forward_flat, preferred_element_type=jnp.float32)
    spectra = spectra.astype(jnp.bfloat16).reshape(slot_count, wave_count, 2, normed.shape[2])
    received = lax.all_to_all(spectra, "lat", split_axis=1, concat_axis=0, tiled=True)
    own_waves = lax.dynamic_slice_in_dim(owner_wavenumber, my_index * wave_share, wave_share)
    degree_mask = (jnp.arange(degrees, dtype=jnp.int32)[None, :] >= own_waves[:, None]).astype(
        jnp.float32
    )
    padded_table = jnp.where(
        slot_valid[None, :, None],
        jnp.take(legendre, slot_live, axis=1),
        jnp.zeros((), jnp.bfloat16),
    )
    slot_weight = jnp.where(slot_valid, jnp.take(quad_weight, slot_live), 0.0)
    weighted = (received.astype(jnp.float32) * slot_weight[:, None, None, None]).astype(
        jnp.bfloat16
    )
    coefficient = jnp.einsum(
        "rsl,srtc->rltc", padded_table, weighted, preferred_element_type=jnp.float32
    )
    filtered = (
        coefficient * degree_mask[:, :, None, None] * spectral_gain[None, :, None, :]
    ).astype(jnp.bfloat16)
    mixed = jnp.dot(filtered.reshape(-1, channels), channel_mix, preferred_element_type=jnp.float32)
    mixed = mixed.astype(jnp.bfloat16).reshape(wave_share, degrees, 2, channels)
    outgoing = jnp.einsum(
        "rsl,rltc->srtc", padded_table, mixed, preferred_element_type=jnp.float32
    ).astype(jnp.bfloat16)
    inverse_flat = inverse_table(owner_wavenumber, longitudes).reshape(2 * wave_count, longitudes)
    returned = lax.all_to_all(outgoing, "lat", split_axis=0, concat_axis=1, tiled=True)
    flat_back = returned.reshape(slot_count, 2 * wave_count, returned.shape[3])
    return jnp.einsum(
        "sqc,qk->skc", flat_back, inverse_flat, preferred_element_type=jnp.float32
    ).astype(jnp.bfloat16)


def solution(mesh):
    return jax.shard_map(
        body,
        mesh=mesh,
        in_specs=(P(("group", "lat"), None, None), P(), P(), P("lat", None, None), P(), P(), P()),
        out_specs=P(("group", "lat"), None, None),
        check_vma=False,
    )
```

profile of v0, /device:TPU:37, one launch (start us, length us, event | category | flops | bytes accessed | tf_op | source)
XLA Modules:
  0.0 688.8 jit_solution(1582650635942233644)
XLA Ops:
  7.4 4.8 fusion.1
  12.9 35.0 %all-to-all-start = ((f32[64,1,512]{2,1,0:T(1,128)}), f32[64,1,512]{2,1,0:T(1,128)S(1)}, u32[]{:S(2)}, u32[]{:S(2)}) async-start(f32[64,1,512]{2,1,0:T(1,128)} %broadcast_in_dim.90), calls=%async_computation | async-start | bytes 262144 | tf_op jit(solution)/shard_map/all_to_all | solution.py:11
  47.9 10.0 %multiply_convert_fusion.4 = (bf16[384,1,1440]{0,2,1:T(8,128)(2,1)S(1)}, bf16[384,1,1440]{0,2,1:T(8,128)(2,1)S(1)}, bf16[384,1,1440]{0,2,1:T(8,128)(2,1)S(1)}, bf16[384,1,1440]{0,2,1:T(8,128)(2,1)S(1)}) fusion(f32[384]{0:T(512)S(1)} %select_multiply_fusion, s32[384]{0:T(512)S(1)} %copy-done.4), kind=kLoop, calls=%fused_computation.37 | loop fusion | flops 9953280 | bytes 4426752 | tf_op jit(solution)/shard_map/convert.5
  60.4 6.8 copy.65
  67.2 6.0 convert_element_type.97
  73.2 4.7 all-to-all-done
  78.1 9.3 %convert_bitcast_fusion.2 = bf16[7,768,256]{2,1,0:T(8,128)(2,1)} fusion(bf16[7,1440,256]{2,1,0:T(8,128)(2,1)} %param.7, f32[256]{0:T(256)S(1)} %get-tuple-element.17, f32[256]{0:T(256)S(1)} %get-tuple-element.16, f32[7]{0:T(128)S(1)} %dynamic-slice_convert_fusion, bf16[768,1440]{1,0:T(8,128)(2,1)} %convert_element_type.97), kind=kOutput, calls=%fused_computation.24 | convolution fusion | flops 3977895936 | bytes 10127388 | tf_op jit(solution)/shard_map/skc,qk->sqc/dot_general | solution.py:93
  87.4 6.5 reshape.383
  93.9 5.2 copy.68
  99.1 19.4 %all-to-all-start.1 = ((bf16[7,384,2,256]{3,2,0,1:T(2,128)(2,1)}), bf16[7,384,2,256]{3,2,0,1:T(2,128)(2,1)}, u32[]{:S(2)}, u32[]{:S(2)}) async-start(bf16[7,384,2,256]{3,2,0,1:T(2,128)(2,1)} %copy.68), calls=%async_computation.1 | async-start | bytes 5505024 | tf_op jit(solution)/shard_map/all_to_all | solution.py:95
  118.6 9.0 %gather_fusion = bf16[448,6,384]{2,0,1:T(8,128)(2,1)} fusion(bf16[6,384,384]{2,1,0:T(8,128)(2,1)S(1)} %copy-done, s32[1024]{0:T(1024)S(1)} %pad_clamp_fusion), kind=kCustom, calls=%fused_computation | custom fusion | bytes 4130560 | tf_op jit(solution)/shard_map/jit(_take)/gather | solution.py:102
  128.2 241.9 %all-to-all-done.1 = bf16[7,384,2,256]{3,2,0,1:T(2,128)(2,1)} async-done(((bf16[7,384,2,256]{3,2,0,1:T(2,128)(2,1)}), bf16[7,384,2,256]{3,2,0,1:T(2,128)(2,1)}, u32[]{:S(2)}, u32[]{:S(2)}) %all-to-all-start.1) | async-done | bytes 2752544 | tf_op jit(solution)/shard_map/all_to_all | solution.py:95
  372.4 4.2 copy.70
  378.6 3.7 multiply_convert_fusion
  382.3 4.0 copy.73
  386.3 5.1 reshape.384
  393.6 4.9 reshape.385
  401.7 4.4 copy.75
  406.1 10.2 %all-to-all-start.2 = ((bf16[448,6,2,256]{3,2,1,0:T(2,128)(2,1)}), bf16[448,6,2,256]{3,2,1,0:T(2,128)(2,1)S(1)}, u32[]{:S(2)}, u32[]{:S(2)}) async-start(bf16[448,6,2,256]{3,2,1,0:T(2,128)(2,1)} %copy.75), calls=%async_computation.2 | async-start | bytes 5505024 | tf_op jit(solution)/shard_map/all_to_all | solution.py:121
  416.3 6.9 copy.63
  423.1 6.0 convert_element_type.96
  429.2 240.1 %all-to-all-done.2 = bf16[448,6,2,256]{3,2,1,0:T(2,128)(2,1)S(1)} async-done(((bf16[448,6,2,256]{3,2,1,0:T(2,128)(2,1)}), bf16[448,6,2,256]{3,2,1,0:T(2,128)(2,1)S(1)}, u32[]{:S(2)}, u32[]{:S(2)}) %all-to-all-start.2) | async-done | bytes 2752544 | tf_op jit(solution)/shard_map/all_to_all | solution.py:121
  672.7 6.8 reshape.386
  679.4 9.2 %convert_bitcast_fusion = bf16[7,1440,256]{2,1,0:T(8,128)(2,1)} fusion(bf16[7,768,256]{2,1,0:T(8,128)(2,1)} %reshape.386, bf16[768,1440]{1,0:T(8,128)(2,1)} %convert_element_type.96), kind=kOutput, calls=%fused_computation.14 | convolution fusion | flops 3966197760 | bytes 10125312 | tf_op jit(solution)/shard_map/sqc,qk->skc/dot_general | solution.py:123
  (40 shorter events, 24.7 us)
Async XLA Ops:
  0.0 118.6 %copy-start = (bf16[6,384,384]{2,1,0:T(8,128)(2,1)S(1)}, bf16[6,384,384]{2,1,0:T(8,128)(2,1)}, u32[]{:S(2)}) copy-start(bf16[6,384,384]{2,1,0:T(8,128)(2,1)} %param.10) | copy-start | bytes 5308420
  6.8 0.5 copy-start.6
  7.4 40.5 %copy-start.4 = (s32[384]{0:T(512)S(1)}, s32[384]{0:T(512)}, u32[]{:S(2)}) copy-start(s32[384]{0:T(512)} %param.9) | copy-start | bytes 4612
  12.9 65.0 %all-to-all-start = ((f32[64,1,512]{2,1,0:T(1,128)}), f32[64,1,512]{2,1,0:T(1,128)S(1)}, u32[]{:S(2)}, u32[]{:S(2)}) async-start(f32[64,1,512]{2,1,0:T(1,128)} %broadcast_in_dim.90), calls=%async_computation | async-start | bytes 262144 | tf_op jit(solution)/shard_map/all_to_all | solution.py:11
  99.1 271.0 %all-to-all-start.1 = ((bf16[7,384,2,256]{3,2,0,1:T(2,128)(2,1)}), bf16[7,384,2,256]{3,2,0,1:T(2,128)(2,1)}, u32[]{:S(2)}, u32[]{:S(2)}) async-start(bf16[7,384,2,256]{3,2,0,1:T(2,128)(2,1)} %copy.68), calls=%async_computation.1 | async-start | bytes 5505024 | tf_op jit(solution)/shard_map/all_to_all | solution.py:95
  376.7 1.9 copy-start.2
  386.3 5.1 copy-start.3
  393.6 4.9 copy-start.5
  393.6 4.9 copy-start.7
  406.1 263.2 %all-to-all-start.2 = ((bf16[448,6,2,256]{3,2,1,0:T(2,128)(2,1)}), bf16[448,6,2,256]{3,2,1,0:T(2,128)(2,1)S(1)}, u32[]{:S(2)}, u32[]{:S(2)}) async-start(bf16[448,6,2,256]{3,2,1,0:T(2,128)(2,1)} %copy.75), calls=%async_computation.2 | async-start | bytes 5505024 | tf_op jit(solution)/shard_map/all_to_all | solution.py:121
  679.4 9.2 %copy-start.1 = (bf16[6,384,384]{2,1,0:T(8,128)(2,1)S(1)}, bf16[6,384,384]{2,1,0:T(8,128)(2,1)}, u32[]{:S(2)}) copy-start(bf16[6,384,384]{2,1,0:T(8,128)(2,1)} %param.10) | copy-start | bytes 5308420
where the time goes:
time: 697 us; the launch traced here: 689 us
  waiting for transfers between devices  487 us (70%)
  local copies, waits for them, and re-layouts  86.8 us (12%)
  starting transfers between devices  64.6 us (9%)
  matrix products  27.5 us (4%)
  other arithmetic  22.8 us (3%)
    all_to_all x1, waiting for transfers between devices, body(): lax.all_to_all(spectra, 'lat', split_axis=1, concat_axis=0, tiled=True)  242 us
    all_to_all x1, waiting for transfers between devices, body(): lax.all_to_all(outgoing, 'lat', split_axis=0, concat_axis=1, tiled=True)  240 us
    all_to_all x1, starting transfers between devices, from_everyone(): return lax.all_to_all(copies, axis, split_axis=0, concat_axis=0, tiled=True)  35 us
    all_to_all x1, starting transfers between devices, body(): lax.all_to_all(spectra, 'lat', split_axis=1, concat_axis=0, tiled=True)  19.4 us
  transfers between devices with their start and end apart: 3, of which 3 were waited for; matrix products, arithmetic and copies ran while one was open for 7% of the time, Pallas kernels for 0%

commit v1 on v0

v1 whole, which is shorter than its diff:
```python
import functools
import math

import jax
import jax.numpy as jnp
import numpy as np
from jax import lax
from jax.experimental import pallas as pl
from jax.experimental.pallas import tpu as pltpu
from jax.sharding import PartitionSpec as P

MESH = pl.DeviceIdType.MESH
LANES = 128
PAIR = 2
ROWS = 8
BF16, F32 = jnp.bfloat16, jnp.float32


def dot(a, b, contract=(1, 0)):
    return lax.dot_general(
        a, b, (((contract[0],), (contract[1],)), ((), ())), preferred_element_type=F32
    )


def kernel(
    dims,
    counts,
    owner,
    x_hbm,
    leg_hbm,
    coef,
    cos_b,
    sin_b,
    count_rows,
    before,
    mine,
    slot_no,
    quad,
    gain,
    mix,
    out_hbm,
    x,
    leg,
    table,
    acc,
    send,
    recv,
    back_send,
    back_recv,
    flat,
    weighted,
    padded,
    pick,
    row_weight,
    table_sum,
    mixed,
    stat_send,
    stat_recv,
    x_sem,
    leg_sem,
    out_sem,
    send_sem,
    recv_sem,
    back_send_sem,
    back_recv_sem,
    stat_sems,
):
    n, slots, longitudes, chunks, points = dims
    me = lax.axis_index("lat")
    quads = n * PAIR * 2
    padded_points = table.shape[2]
    blocks = padded_points // LANES
    degrees = gain.shape[0]

    def peer_of(step):
        far = n - step
        half = (far + 1) // 2
        return lax.rem(me + half * (1 - 2 * lax.rem(far + 1, 2)) + n, n)

    barrier = pltpu.get_barrier_semaphore()

    def greet(step, carry):
        pl.semaphore_signal(
            barrier, inc=1, device_id={"lat": peer_of(step)}, device_id_type=MESH
        )
        return carry

    lax.fori_loop(1, n, greet, 0)

    def x_copy(s):
        return pltpu.make_async_copy(
            x_hbm.at[s], x.at[s, pl.ds(0, longitudes)], x_sem.at[s]
        )

    for s in range(slots):
        x_copy(s).start()
    leg_copy = pltpu.make_async_copy(leg_hbm, leg, leg_sem)
    leg_copy.start()

    band = 32

    def build(i, carry):
        k, r = i // (quads // band), lax.rem(i, quads // band) * band
        r = pl.multiple_of(r, band)
        at = pl.multiple_of(i * band, band)
        c, cb, sb = (ref[pl.ds(at, band), :] for ref in (coef, cos_b, sin_b))
        for a in range(blocks):
            table[k, pl.ds(r, band), a * LANES : (a + 1) * LANES] = (
                c[:, a : a + 1] * cb + c[:, 16 + a : 17 + a] * sb
            ).astype(BF16)
        return carry

    lax.fori_loop(0, chunks * quads // band, build, 0)

    if padded_points > longitudes:
        x[:, longitudes:, :] = jnp.zeros(
            (slots, padded_points - longitudes, x.shape[2]), BF16
        )
    for s in range(slots):
        x_copy(s).wait()

    def fourier(k):
        start = pl.multiple_of(k * quads, quads)
        residual = coef[pl.ds(start, quads), 32:33]

        def one(s, carry):
            values = dot(table[k], x[s])
            values = values - residual * values.astype(BF16).astype(F32)
            flat[pl.ds(0, quads, stride=2), :] = values[:, :LANES]
            flat[pl.ds(1, quads, stride=2), :] = values[:, LANES:]
            send[k, :, s] = (
                flat[pl.ds(0, 2 * quads), :].reshape(n, ROWS, LANES).astype(BF16)
            )
            return carry

        lax.fori_loop(0, slots, one, 0)
        recv[k, me] = send[k, me]

    def exchange(source, target, send_sems, recv_sems, k):
        def one(step, carry):
            peer = peer_of(step)
            pltpu.make_async_remote_copy(
                source.at[k, peer],
                target.at[k, me],
                send_sems.at[k],
                recv_sems.at[k],
                device_id={"lat": peer},
                device_id_type=MESH,
            ).start()
            return carry

        lax.fori_loop(1, n, one, 0)

    def wait_for(buffer, sem):
        part = buffer.at[pl.ds(0, n - 1)]
        pltpu.make_async_copy(part, part, sem).wait()

    fourier(0)

    live = counts[me]
    step_rows = 16 * math.gcd(longitudes // 16, 6)

    def sums(i, carry):
        first, second = carry
        s = i // (longitudes // step_rows)
        r = pl.multiple_of(lax.rem(i, longitudes // step_rows) * step_rows, step_rows)
        on = jnp.where(s < live, 1.0, 0.0).astype(F32)
        values = x[s, pl.ds(r, step_rows), :].astype(F32) * on
        values = values.reshape(step_rows // 8, 8, values.shape[1])
        return first + jnp.sum(values, axis=0), second + jnp.sum(values * values, axis=0)

    zero = jnp.zeros((8, x.shape[2]), F32)
    first, second = lax.fori_loop(
        0, slots * (longitudes // step_rows), sums, (zero, zero)
    )
    first = jnp.sum(first, axis=0, keepdims=True)
    second = jnp.sum(second, axis=0, keepdims=True)
    for i, part in enumerate(
        (first[:, :LANES], first[:, LANES:], second[:, :LANES], second[:, LANES:])
    ):
        stat_send[i : i + 1, :] = part
    stat_recv[me] = stat_send[...]

    pl.semaphore_wait(barrier, n - 1)

    def send_stats(step, carry):
        peer = peer_of(step)
        pltpu.make_async_remote_copy(
            stat_send,
            stat_recv.at[me],
            stat_sems.at[0],
            stat_sems.at[1],
            device_id={"lat": peer},
            device_id_type=MESH,
        ).start()
        return carry

    lax.fori_loop(1, n, send_stats, 0)
    exchange(send, recv, send_sem, recv_sem, 0)
    for k in range(1, chunks):
        fourier(k)
        exchange(send, recv, send_sem, recv_sem, k)

    leg_copy.wait()
    start = dot(before[...], count_rows[...])[:, :1]
    count = dot(mine[...], count_rows[...])[:, :1]
    latitude = lax.broadcasted_iota(jnp.int32, pick.shape, 1).astype(F32)
    hot = (latitude == start + slot_no[...]) & (slot_no[...] < count)
    hot = jnp.where(hot, 1.0, 0.0).astype(F32)
    pick[...] = hot.astype(BF16)
    row_weight[...] = jnp.broadcast_to(
        jnp.sum(hot * quad[...], axis=1, keepdims=True), row_weight.shape
    )

    def pad(w, carry):
        padded[w] = dot(pick[...], leg[w]).astype(BF16)
        return carry

    lax.fori_loop(0, chunks * PAIR, pad, 0)

    inside = lax.broadcasted_iota(jnp.int32, (padded_points, LANES), 0) < longitudes
    ones = jnp.where(inside, 1.0, 0.0).astype(F32).astype(BF16)

    def sum_table(k, carry):
        table_sum[pl.ds(pl.multiple_of(k * quads, quads), quads), :] = dot(table[k], ones)
        return carry

    lax.fori_loop(0, chunks, sum_table, 0)

    wait_for(stat_recv, stat_sems.at[1])
    totals = jnp.sum(stat_recv[...], axis=0)
    mean = totals[0:2] / points
    variance = totals[2:4] / points - mean * mean
    scale = lax.rsqrt(variance + 1e-05)

    rows = n * slots

    def legendre(k, carry):
        wait_for(recv.at[k], recv_sem.at[k])

        def widen(i, inner):
            at = pl.multiple_of(i * slots * ROWS, ROWS)
            flat[pl.ds(at, slots * ROWS), :] = (
                recv[k, i].astype(F32).reshape(slots * ROWS, LANES)
            )
            return inner

        lax.fori_loop(0, n, widen, 0)

        def wave(w, inner):
            number = owner[me * chunks * PAIR + k * PAIR + w]
            is_zero = jnp.where(number == 0, 1.0, 0.0).astype(F32)
            for h in range(2):
                m_h, s_h = mean[h : h + 1], scale[h : h + 1]
                re = flat[pl.ds(w * 4 + h, rows, stride=ROWS), :]
                im = flat[pl.ds(w * 4 + 2 + h, rows, stride=ROWS), :]
                re = re + is_zero * im
                im = im - is_zero * im
                at = k * quads + me * 2 * PAIR + w * 2
                d_re = table_sum[pl.ds(at, 1), :]
                d_im = table_sum[pl.ds(at + 1, 1), :] * (1.0 - is_zero)
                for t, (value, d) in enumerate(((re, d_re), (im, d_im))):
                    left = (2 * t + h) * LANES
                    weighted[:, left : left + LANES] = (
                        ((value - m_h * d) * s_h) * row_weight[...]
                    ).astype(BF16)
            here = padded[k * PAIR + w]
            coefficient = dot(here, weighted[...], (0, 0))
            keep = lax.broadcasted_iota(jnp.int32, (degrees, 1), 0) >= number
            factor = jnp.where(keep, gain[...], 0.0)
            for t in range(2):
                cols = slice(2 * t * LANES, 2 * (t + 1) * LANES)
                filtered = (coefficient[:, cols] * factor).astype(BF16)
                mixed[:, cols] = dot(filtered, mix[...]).astype(BF16)
            synthesis = dot(here, mixed[...])
            for t in range(2):
                doubled = 2.0 - is_zero if t == 0 else 2.0 - 2.0 * is_zero
                for h in range(2):
                    left = (2 * t + h) * LANES
                    flat[pl.ds(w * 4 + t * 2 + h, rows, stride=ROWS), :] = (
                        synthesis[:, left : left + LANES] * doubled
                    )
            return inner

        lax.fori_loop(0, PAIR, wave, 0)

        def narrow(i, inner):
            at = pl.multiple_of(i * slots * ROWS, ROWS)
            back_send[k, i] = (
                flat[pl.ds(at, slots * ROWS), :].reshape(slots, ROWS, LANES).astype(BF16)
            )
            return inner

        lax.fori_loop(0, n, narrow, 0)
        back_recv[k, me] = back_send[k, me]
        exchange(back_send, back_recv, back_send_sem, back_recv_sem, k)
        return carry

    lax.fori_loop(0, chunks, legendre, 0)

    def spread(k, s):
        flat[pl.ds(0, 2 * quads), :] = (
            back_recv[k, :, s].astype(F32).reshape(2 * quads, LANES)
        )
        halves = [flat[pl.ds(h, quads, stride=2), :].astype(BF16) for h in range(2)]
        return dot(table[k], jnp.concatenate(halves, axis=1), (0, 0))

    def out_copy(s):
        return pltpu.make_async_copy(
            x.at[s, pl.ds(0, longitudes)], out_hbm.at[s], out_sem.at[s]
        )

    for k in range(chunks):
        wait_for(back_recv.at[k], back_recv_sem.at[k])

        def one(s, carry, k=k):
            part = spread(k, s)
            if k > 0:
                part = part + acc[s]
            if k < chunks - 1:
                acc[s] = part
            else:
                x[s] = part.astype(BF16)
                out_copy(s).start()
            return carry

        lax.fori_loop(0, slots, one, 0)

    wait_for(stat_recv, stat_sems.at[0])
    for k in range(chunks):
        wait_for(send.at[k], send_sem.at[k])
        wait_for(back_send.at[k], back_send_sem.at[k])
    for s in range(slots):
        out_copy(s).wait()


def angle_tables(waves, longitudes):
    two_pi, factor = 2.0 * math.pi / longitudes, 1.0 / math.sqrt(longitudes)
    part = jnp.arange(waves.shape[0] * 2, dtype=jnp.int32)[:, None] % 2
    waves = jnp.repeat(waves, 2)[:, None]
    lane = jnp.arange(LANES, dtype=jnp.int32)[None, :]
    fine = (waves * lane % longitudes).astype(F32) * two_pi
    coarse = (waves * ((lane % 16) * LANES % longitudes) % longitudes).astype(F32) * two_pi
    cos_a, sin_a = jnp.cos(coarse) * factor, jnp.sin(coarse) * factor
    first = jnp.where((part == 0) | (waves == 0), cos_a, -sin_a)
    second = jnp.where(part == 0, -sin_a, -cos_a)
    residual = jnp.where((part == 1) & (waves == 0), 1.0, 0.0).astype(F32)
    coef = jnp.where(lane < 16, first, jnp.where(lane < 32, second, residual))
    return coef, jnp.cos(fine), jnp.sin(fine)


def body(
    grid_values, lat_counts, owner_wavenumber, legendre, quad_weight, spectral_gain, channel_mix
):
    slots, longitudes, channels = grid_values.shape
    n = lat_counts.shape[0]
    share, live_total, degrees = legendre.shape
    chunks = share // PAIR
    blocks = -(-longitudes // LANES)
    padded_points = blocks * LANES
    quads = n * PAIR * 2
    rows = n * slots
    ordered = owner_wavenumber.reshape(n, chunks, PAIR).transpose(1, 0, 2).reshape(-1)
    coef, cos_b, sin_b = angle_tables(ordered, longitudes)
    holder = np.arange(rows)[:, None] // slots
    device = np.arange(n)[None, :]
    before = jnp.asarray(device < holder, BF16)
    mine = jnp.asarray(device == holder, BF16)
    slot_no = jnp.asarray(np.arange(rows)[:, None] % slots, F32)
    count_rows = jnp.broadcast_to(lat_counts.astype(BF16)[:, None], (n, LANES))
    smem = pl.BlockSpec(memory_space=pltpu.SMEM)
    vmem = pl.BlockSpec(memory_space=pltpu.VMEM)
    anywhere = pl.BlockSpec(memory_space=pl.ANY)
    message = (chunks, n, slots, ROWS, LANES)
    dma = pltpu.SemaphoreType.DMA
    dims = (n, slots, longitudes, chunks, live_total * longitudes)
    return pl.pallas_call(
        functools.partial(kernel, dims),
        out_shape=jax.ShapeDtypeStruct(grid_values.shape, BF16),
        in_specs=[smem, smem, anywhere, anywhere] + [vmem] * 10,
        out_specs=anywhere,
        scratch_shapes=[
            pltpu.VMEM((slots, padded_points, channels), BF16),
            pltpu.VMEM((share, live_total, degrees), BF16),
            pltpu.VMEM((chunks, quads, padded_points), BF16),
            pltpu.VMEM((slots, padded_points, channels), F32),
            pltpu.VMEM(message, BF16),
            pltpu.VMEM(message, BF16),
            pltpu.VMEM(message, BF16),
            pltpu.VMEM(message, BF16),
            pltpu.VMEM((max(rows * ROWS, 2 * quads), LANES), F32),
            pltpu.VMEM((rows, 2 * channels), BF16),
            pltpu.VMEM((share, rows, degrees), BF16),
            pltpu.VMEM((rows, live_total), BF16),
            pltpu.VMEM((rows, LANES), F32),
            pltpu.VMEM((chunks * quads, LANES), F32),
            pltpu.VMEM((degrees, 2 * channels), BF16),
            pltpu.VMEM((4, LANES), F32),
            pltpu.VMEM((n, 4, LANES), F32),
            dma((slots,)),
            dma,
            dma((slots,)),
            dma((chunks,)),
            dma((chunks,)),
            dma((chunks,)),
            dma((chunks,)),
            dma((2,)),
        ],
        compiler_params=pltpu.CompilerParams(
            collective_id=0, has_side_effects=True, vmem_limit_bytes=60 * 1024 * 1024
        ),
    )(
        lat_counts,
        owner_wavenumber,
        grid_values,
        legendre,
        coef,
        cos_b,
        sin_b,
        count_rows,
        before,
        mine,
        slot_no,
        quad_weight[None, :],
        spectral_gain,
        channel_mix,
    )


def solution(mesh):
    return jax.shard_map(
        body,
        mesh=mesh,
        in_specs=(P(("group", "lat"), None, None), P(), P(), P("lat", None, None), P(), P(), P()),
        out_specs=P(("group", "lat"), None, None),
        check_vma=False,
    )
```

time: 697 us -> 541 us (0.78); the launches traced: 689 us -> 541 us
  Pallas kernels: 0 us -> 527 us
  waiting for transfers between devices: 487 us -> 0 us
  local copies, waits for them, and re-layouts: 86.8 us -> 8.27 us
  starting transfers between devices: 64.6 us -> 0 us
  matrix products: 27.5 us -> 0 us
  other arithmetic: 22.8 us -> 5.47 us
    pallas_call x0 -> x1, Pallas kernels: none -> 527 us  [body(): pl.pallas_call(functools.partial(kernel, dims), out_shape=jax.ShapeDtypeS...]
    all_to_all x3 -> x0, waiting for transfers between devices: 487 us -> none  [the longest x1 242 us: body(): lax.all_to_all(spectra, 'lat', split_axis=1, concat_axis=0, tiled=True)]
    all_to_all x3 -> x0, starting transfers between devices: 64.6 us -> none  [the longest x1 35 us: from_everyone(): return lax.all_to_all(copies, axis, split_axis=0, concat_axis=0, tiled=True)]
    dot_general x5 -> x0, matrix products: 27.5 us -> none  [the longest x1 9.26 us: body(): jnp.einsum('skc,qk->sqc', normed, forward_flat, preferred_element_type=jn...]
    reshape x5 -> x2, local copies, waits for them, and re-layouts: 28.4 us -> 0.98 us  [body(): owner_wavenumber.reshape(n, chunks, PAIR).transpose(1, 0, 2).reshape(-1)]
    convert_element_type x6 -> x0, local copies, waits for them, and re-layouts: 26.5 us -> none  [the longest x2 6.14 us: body(): received.astype(jnp.float32) * slot_weight[:, None, None, None]]
    another operation x3 -> x1, local copies, waits for them, and re-layouts: 14.5 us -> 0.15 us  [angle_tables(): waves = jnp.repeat(waves, 2)[:, None]]
    another operation x4 -> x0, other arithmetic: 12.7 us -> none
  transfers between devices with their start and end apart: 3 -> 0, of which waited for: 3 -> 0; matrix products, arithmetic and copies ran while one was open for 7% -> 0% of each run, Pallas kernels for 0% -> 0%
where the time goes in v1:
time: 541 us
  Pallas kernels  527 us (97%)
  local copies, waits for them, and re-layouts  8.27 us (2%)
  other arithmetic  5.47 us (1%)
    pallas_call x1, Pallas kernels, body(): pl.pallas_call(functools.partial(kernel, dims), out_shape=jax.ShapeDtypeS...  527 us

profile of v1, /device:TPU:37, one launch (start us, length us, event | category | flops | bytes accessed | tf_op | source)
XLA Modules:
  0.0 541.2 jit_solution(15223203079449782409)
XLA Ops:
  0.0 0.7 convert_element_type.11
  0.7 1.2 broadcast_in_dim.68.quad
  1.9 0.7 broadcast_in_dim.67.count_rows
  2.6 0.8 reshape.84
  3.4 0.1 reshape.85
  3.6 0.1 broadcast_in_dim.60
  3.7 0.1 broadcast_in_dim_reshape.3
  3.9 4.8 fusion.6
  8.7 527.4 %shard_map.100 = bf16[7,1440,256]{2,1,0:T(8,128)(2,1)} custom-call(s32[64]{0:T(128)} %counts.1, s32[384]{0:T(512)} %owner.1, bf16[7,1440,256]{2,1,0:T(8,128)(2,1)} %x_hbm.1, bf16[6,384,384]{2,1,0:T(8,128)(2,1)} %leg_hbm.1, f32[768,128]{1,0:T(8,128)} %get-tuple-element.9.coef, f32[768,128]{1,0:T(8,128)} %get-tuple-element.8.cos_b, ...), custom_call_target="tpu_custom_call" | custom-call | tf_op jit(solution)/shard_map/pallas_call | solution.py:377
  536.1 5.1 copy.13
  (5 shorter events, 0.0 us)

commit v2 on v1

v2 whole, which is shorter than its diff:
```python
import functools
import math

import jax
import jax.numpy as jnp
import numpy as np
from jax import lax
from jax.experimental import pallas as pl
from jax.experimental.pallas import tpu as pltpu
from jax.sharding import PartitionSpec as P

MESH = pl.DeviceIdType.MESH
LANES = 128
PAIR = 2
ROWS = 8
BF16, F32 = jnp.bfloat16, jnp.float32


def dot(a, b, contract=(1, 0)):
    return lax.dot_general(
        a, b, (((contract[0],), (contract[1],)), ((), ())), preferred_element_type=F32
    )


def kernel(
    dims,
    counts,
    owner,
    x_hbm,
    waves_hbm,
    leg_hbm,
    number_hbm,
    count_hbm,
    quad_hbm,
    gain_hbm,
    mix_hbm,
    out,
    x,
    waves,
    leg,
    number_row,
    count_row,
    quad,
    gain,
    mix,
    table,
    turned,
    acc,
    send,
    recv,
    back_send,
    back_recv,
    flat,
    weighted,
    padded,
    row_weight,
    table_sum,
    mixed,
    stat_mine,
    stat_pair,
    stat_send,
    stat_recv,
    stat_total,
    x_sem,
    load_sem,
    send_sem,
    recv_sem,
    back_send_sem,
    back_recv_sem,
    pair_sems,
    stat_sems,
    total_sems,
):
    n, slots, longitudes, chunks, points = dims
    me = lax.axis_index("lat")
    quads = n * PAIR * 2
    half_points = longitudes // 2
    padded_half = table.shape[2] // 2
    padded_points = 2 * padded_half
    degrees = gain.shape[0]
    chips, chip, core = n // 2, me // 2, lax.rem(me, 2)
    partner = me + 1 - 2 * core
    last = chunks - 1
    early = slots - 1

    def ring(here, size, step):
        far = size - step
        half = (far + 1) // 2
        return lax.rem(here + half * (1 - 2 * lax.rem(far + 1, 2)) + size, size)

    def peer_of(step):
        return ring(me, n, step)

    barrier = pltpu.get_barrier_semaphore()

    def greet(step, carry):
        pl.semaphore_signal(
            barrier, inc=1, device_id={"lat": peer_of(step)}, device_id_type=MESH
        )
        return carry

    lax.fori_loop(1, n, greet, 0)

    loads = [
        pltpu.make_async_copy(source, target, load_sem.at[i])
        for i, (source, target) in enumerate(
            (
                (number_hbm, number_row),
                (waves_hbm, waves),
                (leg_hbm, leg),
                (count_hbm, count_row),
                (quad_hbm, quad),
                (gain_hbm, gain),
                (mix_hbm, mix),
            )
        )
    ]

    def x_copy(s, h):
        return pltpu.make_async_copy(
            x_hbm.at[s, pl.ds(h * half_points, half_points)],
            x.at[s, pl.ds(h * padded_half, half_points)],
            x_sem.at[s, h],
        )

    halves = [(s, h) for s in range(slots) for h in range(2)]
    for load in loads[:2]:
        load.start()
    for s, h in halves:
        x_copy(s, h).start()
    for load in loads[2:]:
        load.start()

    if padded_half > half_points:
        for h in range(2):
            x[:, h * padded_half + half_points : (h + 1) * padded_half, :] = jnp.zeros(
                (slots, padded_half - half_points, x.shape[2]), BF16
            )
    for load in loads[:2]:
        load.wait()

    def build(k):
        q, r = (lax.broadcasted_iota(jnp.int32, (quads, LANES), i) for i in range(2))
        slot = (q // (2 * PAIR)) * (chunks * PAIR) + k * PAIR + lax.rem(q // 2, PAIR)
        held = jnp.zeros((quads, LANES), F32)
        for i in range(number_row.shape[0]):
            numbers = number_row[i : i + 1, :].astype(F32)
            held = held + jnp.where(slot == r + i * LANES, numbers, 0.0)
        part = lax.rem(lax.broadcasted_iota(jnp.int32, (quads, 1), 0), 2).astype(F32)
        code = 2.0 * jnp.sum(held, axis=1, keepdims=True) + part
        column = lax.broadcasted_iota(jnp.int32, (quads, waves.shape[0]), 1).astype(F32)
        hot = jnp.where(column == code, 1.0, 0.0).astype(F32).astype(BF16)
        rows = dot(hot, waves[...])
        first, sign = rows[:, :padded_half], rows[:, padded_half : padded_half + 1]
        table[k, :, :padded_half] = first.astype(BF16)
        table[k, :, padded_half:] = (first * sign).astype(BF16)
        return rows[:, padded_half + 1 : padded_half + 2]

    def fourier(k):
        residual = build(k)

        def one(s, carry):
            if k == 0:
                for h in range(2):
                    x_copy(s, h).wait()
            values = dot(table[k], x[s])
            values = values - residual * values.astype(BF16).astype(F32)
            flat[pl.ds(0, quads, stride=2), :] = values[:, :LANES]
            flat[pl.ds(1, quads, stride=2), :] = values[:, LANES:]
            send[k, :, s] = (
                flat[pl.ds(0, 2 * quads), :].reshape(n, ROWS, LANES).astype(BF16)
            )
            return carry

        lax.fori_loop(0, slots, one, 0)
        recv[k, me] = send[k, me]

    def exchange(source, target, send_sems, recv_sems, k, part=None, at=None):
        def cut(ref, i):
            return ref.at[k, i] if part is None else ref.at[k, i, pl.ds(*part)]

        at = k if at is None else at

        def one(step, carry):
            peer = peer_of(step)
            pltpu.make_async_remote_copy(
                cut(source, peer),
                cut(target, me),
                send_sems.at[at],
                recv_sems.at[at],
                device_id={"lat": peer},
                device_id_type=MESH,
            ).start()
            return carry

        lax.fori_loop(1, n, one, 0)

    def wait_for(buffer, sem):
        pltpu.make_async_copy(buffer, buffer, sem).wait()

    def others(buffer, k):
        return buffer.at[k, pl.ds(0, n - 1)]

    fourier(0)
    pl.semaphore_wait(barrier, n - 1)
    exchange(send, recv, send_sem, recv_sem, 0)

    live = counts[me]
    step_rows = 96

    def sums(i, carry):
        first, second = carry
        s = i // (padded_points // step_rows)
        r = pl.multiple_of(lax.rem(i, padded_points // step_rows) * step_rows, step_rows)
        on = jnp.where(s < live, 1.0, 0.0).astype(F32)
        values = x[s, pl.ds(r, step_rows), :].astype(F32) * on
        values = values.reshape(step_rows // 8, 8, values.shape[1])
        return first + jnp.sum(values, axis=0), second + jnp.sum(values * values, axis=0)

    zero = jnp.zeros((8, x.shape[2]), F32)
    first, second = lax.fori_loop(
        0, slots * (padded_points // step_rows), sums, (zero, zero)
    )
    first = jnp.sum(first, axis=0, keepdims=True)
    second = jnp.sum(second, axis=0, keepdims=True)
    for i, part in enumerate((first, second)):
        for h in range(2):
            stat_mine[i, h : h + 1, :] = part[:, h * LANES : (h + 1) * LANES]

    def pair_copy(source, target, sems):
        return pltpu.make_async_remote_copy(
            source, target, sems.at[0], sems.at[1], device_id={"lat": partner}, device_id_type=MESH
        )

    to_partner = pair_copy(stat_mine.at[1 - core], stat_pair, pair_sems)
    to_partner.start()
    for k in range(1, chunks):
        fourier(k)
        if k == 1:
            to_partner.wait()
            stat_send[...] = stat_mine[core] + stat_pair[...]
            stat_recv[chip] = stat_send[...]

            def send_stats(step, carry):
                pltpu.make_async_remote_copy(
                    stat_send,
                    stat_recv.at[chip],
                    stat_sems.at[0],
                    stat_sems.at[1],
                    device_id={"lat": ring(chip, chips, step) * 2 + core},
                    device_id_type=MESH,
                ).start()
                return carry

            lax.fori_loop(1, chips, send_stats, 0)
        exchange(send, recv, send_sem, recv_sem, k)

    for load in loads[2:]:
        load.wait()
    row = lax.broadcasted_iota(jnp.int32, (n * slots, n), 0)
    device = lax.broadcasted_iota(jnp.int32, (n * slots, n), 1)
    holder, slot_no = row // slots, lax.rem(row[:, :1], slots).astype(F32)
    number_live = count_row[...].astype(F32)
    start = jnp.sum(jnp.where(device < holder, number_live, 0.0), axis=1, keepdims=True)
    count = jnp.sum(jnp.where(device == holder, number_live, 0.0), axis=1, keepdims=True)
    latitude = lax.broadcasted_iota(jnp.int32, (n * slots, leg.shape[1]), 1).astype(F32)
    hot = (latitude == start + slot_no) & (slot_no < count)
    hot = jnp.where(hot, 1.0, 0.0).astype(F32)
    held = jnp.zeros(row_weight.shape, F32)
    for i in range(quad.shape[0]):
        held = held + hot[:, i * LANES : (i + 1) * LANES] * quad[i : i + 1, :]
    row_weight[...] = jnp.broadcast_to(
        jnp.sum(held, axis=1, keepdims=True), row_weight.shape
    )
    pick = hot.astype(BF16)

    def pad(w, carry):
        padded[w] = dot(pick, leg[w]).astype(BF16)
        return carry

    lax.fori_loop(0, chunks * PAIR, pad, 0)

    point = lax.rem(lax.broadcasted_iota(jnp.int32, (padded_points, LANES), 0), padded_half)
    ones = jnp.where(point < half_points, 1.0, 0.0).astype(F32).astype(BF16)

    def sum_table(k, carry):
        table_sum[pl.ds(pl.multiple_of(k * quads, quads), quads), :] = dot(table[k], ones)
        return carry

    lax.fori_loop(0, chunks, sum_table, 0)
    r, c = (lax.broadcasted_iota(jnp.int32, (quads, quads), i) for i in range(2))
    unit = jnp.where(r == c, 1.0, 0.0).astype(F32).astype(BF16)
    turned[...] = dot(table[last], unit, (0, 0)).astype(BF16)

    wait_for(stat_recv.at[pl.ds(0, chips - 1)], stat_sems.at[1])
    stat_total[core] = jnp.sum(stat_recv[...], axis=0)
    total_copy = pair_copy(stat_total.at[core], stat_total.at[core], total_sems)
    total_copy.start()
    total_copy.wait()
    mean = stat_total[0] / points
    variance = stat_total[1] / points - mean * mean
    scale = lax.rsqrt(variance + 1e-05)

    rows = n * slots

    def legendre(k, carry):
        wait_for(others(recv, k), recv_sem.at[k])

        def widen(i, inner):
            at = pl.multiple_of(i * slots * ROWS, ROWS)
            flat[pl.ds(at, slots * ROWS), :] = (
                recv[k, i].astype(F32).reshape(slots * ROWS, LANES)
            )
            return inner

        lax.fori_loop(0, n, widen, 0)

        def wave(w, inner):
            number = owner[me * chunks * PAIR + k * PAIR + w]
            is_zero = jnp.where(number == 0, 1.0, 0.0).astype(F32)
            for h in range(2):
                m_h, s_h = mean[h : h + 1], scale[h : h + 1]
                re = flat[pl.ds(w * 4 + h, rows, stride=ROWS), :]
                im = flat[pl.ds(w * 4 + 2 + h, rows, stride=ROWS), :]
                re = re + is_zero * im
                im = im - is_zero * im
                at = k * quads + me * 2 * PAIR + w * 2
                d_re = table_sum[pl.ds(at, 1), :]
                d_im = table_sum[pl.ds(at + 1, 1), :] * (1.0 - is_zero)
                for t, (value, d) in enumerate(((re, d_re), (im, d_im))):
                    left = (2 * t + h) * LANES
                    weighted[:, left : left + LANES] = (
                        ((value - m_h * d) * s_h) * row_weight[...]
                    ).astype(BF16)
            here = padded[k * PAIR + w]
            coefficient = dot(here, weighted[...], (0, 0))
            keep = lax.broadcasted_iota(jnp.int32, (degrees, 1), 0) >= number
            factor = jnp.where(keep, gain[...], 0.0)
            for t in range(2):
                cols = slice(2 * t * LANES, 2 * (t + 1) * LANES)
                filtered = (coefficient[:, cols] * factor).astype(BF16)
                mixed[:, cols] = dot(filtered, mix[...]).astype(BF16)
            synthesis = dot(here, mixed[...])
            for t in range(2):
                doubled = 2.0 - is_zero if t == 0 else 2.0 - 2.0 * is_zero
                for h in range(2):
                    left = (2 * t + h) * LANES
                    flat[pl.ds(w * 4 + t * 2 + h, rows, stride=ROWS), :] = (
                        synthesis[:, left : left + LANES] * doubled
                    )
            return inner

        lax.fori_loop(0, PAIR, wave, 0)

        def narrow(i, inner):
            at = pl.multiple_of(i * slots * ROWS, ROWS)
            back_send[k, i] = (
                flat[pl.ds(at, slots * ROWS), :].reshape(slots, ROWS, LANES).astype(BF16)
            )
            return inner

        lax.fori_loop(0, n, narrow, 0)
        back_recv[k, me] = back_send[k, me]
        return carry

    def legendre_and_return(k, carry):
        legendre(k, carry)
        exchange(back_send, back_recv, back_send_sem, back_recv_sem, k)
        return carry

    lax.fori_loop(0, last, legendre_and_return, 0)
    legendre(last, 0)
    parts = ((0, early), (early, slots - early))
    for i, part in enumerate(parts):
        exchange(back_send, back_recv, back_send_sem, back_recv_sem, last, part, last + i)

    def spread(k, s):
        flat[pl.ds(0, 2 * quads), :] = (
            back_recv[k, :, s].astype(F32).reshape(2 * quads, LANES)
        )
        both = [flat[pl.ds(h, quads, stride=2), :].astype(BF16) for h in range(2)]
        return jnp.concatenate(both, axis=1)

    for k in range(last):
        wait_for(others(back_recv, k), back_recv_sem.at[k])

        def add(s, carry, k=k):
            part = dot(table[k], spread(k, s), (0, 0))
            acc[s] = part if k == 0 else part + acc[s]
            return carry

        lax.fori_loop(0, slots, add, 0)

    def finish(s, carry):
        total = dot(turned[...], spread(last, s)) + acc[s]
        for h in range(2):
            out[s, h * half_points : (h + 1) * half_points, :] = total[
                h * padded_half : h * padded_half + half_points
            ].astype(BF16)
        return carry

    def piece(buffer, part):
        return buffer.at[last, pl.ds(0, n - 1), pl.ds(*part)]

    for k in range(chunks):
        wait_for(others(send, k), send_sem.at[k])
    for k in range(last):
        wait_for(others(back_send, k), back_send_sem.at[k])
    wait_for(stat_recv.at[pl.ds(0, chips - 1)], stat_sems.at[0])
    for i, (first_slot, size) in enumerate(parts):
        wait_for(piece(back_recv, parts[i]), back_recv_sem.at[last + i])
        lax.fori_loop(first_slot, first_slot + size, finish, 0)
    for i, part in enumerate(parts):
        wait_for(piece(back_send, part), back_send_sem.at[last + i])


def wave_rows(wave_count, longitudes, padded_half):
    half = longitudes // 2
    number = np.arange(wave_count)
    phase = number[:, None] * np.arange(half)[None, :] % longitudes
    angle = phase * (2.0 * math.pi / longitudes)
    sine = np.where(number[:, None] > 0, -np.sin(angle), np.cos(angle))
    rows = np.zeros((wave_count, 2, padded_half + LANES), np.float32)
    rows[:, :, :half] = np.stack([np.cos(angle), sine], axis=1) / math.sqrt(longitudes)
    rows[:, :, padded_half] = 1.0 - 2.0 * (number % 2)[:, None]
    rows[0, 1, padded_half + 1] = 1.0
    return jnp.asarray(rows.reshape(2 * wave_count, -1), BF16)


def body(
    grid_values, lat_counts, owner_wavenumber, legendre, quad_weight, spectral_gain, channel_mix
):
    slots, longitudes, channels = grid_values.shape
    n = lat_counts.shape[0]
    share, live_total, degrees = legendre.shape
    chunks = share // PAIR
    padded_half = -(-longitudes // (2 * 256)) * 256
    padded_points = 2 * padded_half
    quads = n * PAIR * 2
    rows = n * slots
    waves = wave_rows(owner_wavenumber.shape[0], longitudes, padded_half)
    smem = pl.BlockSpec(memory_space=pltpu.SMEM)
    anywhere = pl.BlockSpec(memory_space=pl.ANY)
    message = (chunks, n, slots, ROWS, LANES)
    dma = pltpu.SemaphoreType.DMA
    dims = (n, slots, longitudes, chunks, live_total * longitudes)
    return pl.pallas_call(
        functools.partial(kernel, dims),
        out_shape=pltpu.VMEM(grid_values.shape, BF16),
        in_specs=[smem, smem] + [anywhere] * 8,
        out_specs=pl.BlockSpec(memory_space=pltpu.VMEM),
        scratch_shapes=[
            pltpu.VMEM((slots, padded_points, channels), BF16),
            pltpu.VMEM(waves.shape, BF16),
            pltpu.VMEM((share, live_total, degrees), BF16),
            pltpu.VMEM((owner_wavenumber.shape[0] // LANES, LANES), jnp.int32),
            pltpu.VMEM((1, n), jnp.int32),
            pltpu.VMEM((live_total // LANES, LANES), F32),
            pltpu.VMEM((degrees, channels), F32),
            pltpu.VMEM((channels, channels), BF16),
            pltpu.VMEM((chunks, quads, padded_points), BF16),
            pltpu.VMEM((padded_points, quads), BF16),
            pltpu.VMEM((slots, padded_points, channels), F32),
            pltpu.VMEM(message, BF16),
            pltpu.VMEM(message, BF16),
            pltpu.VMEM(message, BF16),
            pltpu.VMEM(message, BF16),
            pltpu.VMEM((max(rows * ROWS, 2 * quads), LANES), F32),
            pltpu.VMEM((rows, 2 * channels), BF16),
            pltpu.VMEM((share, rows, degrees), BF16),
            pltpu.VMEM((rows, LANES), F32),
            pltpu.VMEM((chunks * quads, LANES), F32),
            pltpu.VMEM((degrees, 2 * channels), BF16),
            pltpu.VMEM((2, 2, LANES), F32),
            pltpu.VMEM((2, LANES), F32),
            pltpu.VMEM((2, LANES), F32),
            pltpu.VMEM((n // 2, 2, LANES), F32),
            pltpu.VMEM((2, 2, LANES), F32),
            dma((slots, 2)),
            dma((7,)),
            dma((chunks,)),
            dma((chunks,)),
            dma((chunks + 1,)),
            dma((chunks + 1,)),
            dma((2,)),
            dma((2,)),
            dma((2,)),
        ],
        compiler_params=pltpu.CompilerParams(
            collective_id=0, has_side_effects=True, vmem_limit_bytes=54 * 1024 * 1024
        ),
    )(
        lat_counts,
        owner_wavenumber,
        grid_values,
        waves,
        legendre,
        owner_wavenumber.reshape(-1, LANES),
        lat_counts[None, :],
        quad_weight.reshape(-1, LANES),
        spectral_gain,
        channel_mix,
    )


def solution(mesh):
    return jax.shard_map(
        body,
        mesh=mesh,
        in_specs=(P(("group", "lat"), None, None), P(), P(), P("lat", None, None), P(), P(), P()),
        out_specs=P(("group", "lat"), None, None),
        check_vma=False,
    )
```

time: 541 us -> 515 us (0.952)
  Pallas kernels: 527 us -> 512 us
  local copies, waits for them, and re-layouts: 8.27 us -> 2.33 us
  other arithmetic: 5.47 us -> 0 us
    pallas_call x1, Pallas kernels: 527 us -> 512 us  [body(): pl.pallas_call(functools.partial(kernel, dims), out_shape=pltpu.VMEM(grid...]
where the time goes in v2:
time: 515 us
  Pallas kernels  512 us (99%)
    pallas_call x1, Pallas kernels, body(): pl.pallas_call(functools.partial(kernel, dims), out_shape=pltpu.VMEM(grid...  512 us

profile of v2, /device:TPU:37, one launch (start us, length us, event | category | flops | bytes accessed | tf_op | source)
XLA Modules:
  0.0 514.5 jit_solution(6514046725156225813)
XLA Ops:
  0.0 512.2 %shard_map.82 = bf16[7,1440,256]{2,1,0:T(8,128)(2,1)S(1)} custom-call(s32[64]{0:T(128)} %counts.1, s32[384]{0:T(512)} %owner.1, bf16[7,1440,256]{2,1,0:T(8,128)(2,1)} %x_hbm.1, bf16[768,896]{1,0:T(8,128)(2,1)} %constant.2.clone.waves_hbm, bf16[6,384,384]{2,1,0:T(8,128)(2,1)} %leg_hbm.1, s32[3,128]{1,0:T(4,128)} %bitcast.3, s32[1,64]{1,0:T(1,128)} %bitcast.5, ...), custom_call_target="tpu_custom_call" | custom-call | tf_op jit(solution)/shard_map/pallas_call | solution.py:447
  512.2 2.3 copy.10

commit v3 on v2

--- a/solution.py
+++ b/solution.py
@@ -60,6 +60,8 @@
     stat_pair,
     stat_send,
     stat_recv,
+    block_send,
+    block_recv,
     stat_total,
     x_sem,
     load_sem,
@@ -69,7 +71,9 @@
     back_recv_sem,
     pair_sems,
     stat_sems,
+    block_sems,
     total_sems,
+    far_sem,
 ):
     n, slots, longitudes, chunks, points = dims
     me = lax.axis_index("lat")
@@ -92,6 +96,7 @@
         return ring(me, n, step)
 
     barrier = pltpu.get_barrier_semaphore()
+    near_from = n - n // 2
 
     def greet(step, carry):
         pl.semaphore_signal(
@@ -99,7 +104,7 @@
         )
         return carry
 
-    lax.fori_loop(1, n, greet, 0)
+    lax.fori_loop(near_from, n, greet, 0)
 
     loads = [
         pltpu.make_async_copy(source, target, load_sem.at[i])
@@ -172,10 +177,18 @@
             )
             return carry
 
-        lax.fori_loop(0, slots, one, 0)
+        cut = slots - 2 if k == 0 else slots
+        lax.fori_loop(0, cut, one, 0)
+        if k == 0:
+            pl.semaphore_wait(barrier, n // 2)
+            for edge in (n // 4, n - n // 4):
+                pl.semaphore_signal(
+                    far_sem, inc=1, device_id={"lat": lax.rem(me + edge, n)}, device_id_type=MESH
+                )
+        lax.fori_loop(cut, slots, one, 0)
         recv[k, me] = send[k, me]
 
-    def exchange(source, target, send_sems, recv_sems, k, part=None, at=None):
+    def exchange(source, target, send_sems, recv_sems, k, part=None, at=None, steps=(1, n)):
         def cut(ref, i):
             return ref.at[k, i] if part is None else ref.at[k, i, pl.ds(*part)]
 
@@ -193,7 +206,7 @@
             ).start()
             return carry
 
-        lax.fori_loop(1, n, one, 0)
+        lax.fori_loop(*steps, one, 0)
 
     def wait_for(buffer, sem):
         pltpu.make_async_copy(buffer, buffer, sem).wait()
@@ -202,8 +215,9 @@
         return buffer.at[k, pl.ds(0, n - 1)]
 
     fourier(0)
-    pl.semaphore_wait(barrier, n - 1)
-    exchange(send, recv, send_sem, recv_sem, 0)
+    exchange(send, recv, send_sem, recv_sem, 0, steps=(near_from, n))
+    pl.semaphore_wait(far_sem, 2)
+    exchange(send, recv, send_sem, recv_sem, 0, steps=(1, near_from))
 
     live = counts[me]
     step_rows = 96
@@ -232,6 +246,23 @@
             source, target, sems.at[0], sems.at[1], device_id={"lat": partner}, device_id_type=MESH
         )
 
+    block = stat_recv.shape[0]
+    rank, lane = chip // block, lax.rem(chip, block)
+
+    def stat_copies(source, target, here, size, chip_of, sems):
+        def one(step, carry):
+            pltpu.make_async_remote_copy(
+                source,
+                target.at[here],
+                sems.at[0],
+                sems.at[1],
+                device_id={"lat": chip_of(ring(here, size, step)) * 2 + core},
+                device_id_type=MESH,
+            ).start()
+            return carry
+
+        lax.fori_loop(1, size, one, 0)
+
     to_partner = pair_copy(stat_mine.at[1 - core], stat_pair, pair_sems)
     to_partner.start()
     for k in range(1, chunks):
@@ -239,20 +270,15 @@
         if k == 1:
             to_partner.wait()
             stat_send[...] = stat_mine[core] + stat_pair[...]
-            stat_recv[chip] = stat_send[...]
-
-            def send_stats(step, carry):
-                pltpu.make_async_remote_copy(
-                    stat_send,
-                    stat_recv.at[chip],
-                    stat_sems.at[0],
-                    stat_sems.at[1],
-                    device_id={"lat": ring(chip, chips, step) * 2 + core},
-                    device_id_type=MESH,
-                ).start()
-                return carry
-
-            lax.fori_loop(1, chips, send_stats, 0)
+            stat_recv[lane] = stat_send[...]
+            stat_copies(stat_send, stat_recv, lane, block, lambda i: rank * block + i, stat_sems)
+        if k == last:
+            wait_for(stat_recv.at[pl.ds(0, block - 1)], stat_sems.at[1])
+            block_send[...] = jnp.sum(stat_recv[...], axis=0)
+            block_recv[rank] = block_send[...]
+            stat_copies(
+                block_send, block_recv, rank, chips // block, lambda i: i * block + lane, block_sems
+            )
         exchange(send, recv, send_sem, recv_sem, k)
 
     for load in loads[2:]:
@@ -292,8 +318,8 @@
     unit = jnp.where(r == c, 1.0, 0.0).astype(F32).astype(BF16)
     turned[...] = dot(table[last], unit, (0, 0)).astype(BF16)
 
-    wait_for(stat_recv.at[pl.ds(0, chips - 1)], stat_sems.at[1])
-    stat_total[core] = jnp.sum(stat_recv[...], axis=0)
+    wait_for(block_recv.at[pl.ds(0, chips // block - 1)], block_sems.at[1])
+    stat_total[core] = jnp.sum(block_recv[...], axis=0)
     total_copy = pair_copy(stat_total.at[core], stat_total.at[core], total_sems)
     total_copy.start()
     total_copy.wait()
@@ -406,7 +432,8 @@
         wait_for(others(send, k), send_sem.at[k])
     for k in range(last):
         wait_for(others(back_send, k), back_send_sem.at[k])
-    wait_for(stat_recv.at[pl.ds(0, chips - 1)], stat_sems.at[0])
+    wait_for(stat_recv.at[pl.ds(0, block - 1)], stat_sems.at[0])
+    wait_for(block_recv.at[pl.ds(0, chips // block - 1)], block_sems.at[0])
     for i, (first_slot, size) in enumerate(parts):
         wait_for(piece(back_recv, parts[i]), back_recv_sem.at[last + i])
         lax.fori_loop(first_slot, first_slot + size, finish, 0)
@@ -443,6 +470,7 @@
     anywhere = pl.BlockSpec(memory_space=pl.ANY)
     message = (chunks, n, slots, ROWS, LANES)
     dma = pltpu.SemaphoreType.DMA
+    block = 4 if n // 2 % 4 == 0 else 1
     dims = (n, slots, longitudes, chunks, live_total * longitudes)
     return pl.pallas_call(
         functools.partial(kernel, dims),
@@ -474,7 +502,9 @@
             pltpu.VMEM((2, 2, LANES), F32),
             pltpu.VMEM((2, LANES), F32),
             pltpu.VMEM((2, LANES), F32),
-            pltpu.VMEM((n // 2, 2, LANES), F32),
+            pltpu.VMEM((block, 2, LANES), F32),
+            pltpu.VMEM((2, LANES), F32),
+            pltpu.VMEM((n // 2 // block, 2, LANES), F32),
             pltpu.VMEM((2, 2, LANES), F32),
             dma((slots, 2)),
             dma((7,)),
@@ -485,6 +515,8 @@
             dma((2,)),
             dma((2,)),
             dma((2,)),
+            dma((2,)),
+            pltpu.SemaphoreType.REGULAR,
         ],
         compiler_params=pltpu.CompilerParams(
             collective_id=0, has_side_effects=True, vmem_limit_bytes=54 * 1024 * 1024

time: 515 us -> 510 us (level)
  no operation moved by 1% of the time
where the time goes in v3:
time: 510 us
  Pallas kernels  508 us (100%)
    pallas_call x1, Pallas kernels, body(): pl.pallas_call(functools.partial(kernel, dims), out_shape=pltpu.VMEM(grid...  508 us

profile of v3, /device:TPU:37, one launch (start us, length us, event | category | flops | bytes accessed | tf_op | source)
XLA Modules:
  0.0 510.1 jit_solution(14073510636360162128)
XLA Ops:
  0.0 507.8 %shard_map.82 = bf16[7,1440,256]{2,1,0:T(8,128)(2,1)S(1)} custom-call(s32[64]{0:T(128)} %counts.1, s32[384]{0:T(512)} %owner.1, bf16[7,1440,256]{2,1,0:T(8,128)(2,1)} %x_hbm.1, bf16[768,896]{1,0:T(8,128)(2,1)} %constant.2.clone.waves_hbm, bf16[6,384,384]{2,1,0:T(8,128)(2,1)} %leg_hbm.1, s32[3,128]{1,0:T(4,128)} %bitcast.3, s32[1,64]{1,0:T(1,128)} %bitcast.5, ...), custom_call_target="tpu_custom_call" | custom-call | tf_op jit(solution)/shard_map/pallas_call | solution.py:475
  507.8 2.3 copy.10

commit v4 on v3

--- a/solution.py
+++ b/solution.py
@@ -24,8 +24,6 @@
 
 def kernel(
     dims,
-    counts,
-    owner,
     x_hbm,
     waves_hbm,
     leg_hbm,
@@ -112,8 +110,8 @@
             (
                 (number_hbm, number_row),
                 (waves_hbm, waves),
+                (count_hbm, count_row),
                 (leg_hbm, leg),
-                (count_hbm, count_row),
                 (quad_hbm, quad),
                 (gain_hbm, gain),
                 (mix_hbm, mix),
@@ -188,22 +186,28 @@
         lax.fori_loop(cut, slots, one, 0)
         recv[k, me] = send[k, me]
 
-    def exchange(source, target, send_sems, recv_sems, k, part=None, at=None, steps=(1, n)):
-        def cut(ref, i):
+    def exchange(source, target, send_sems, recv_sems, k, parts=None, only=None, steps=(1, n)):
+        def cut(ref, i, part):
             return ref.at[k, i] if part is None else ref.at[k, i, pl.ds(*part)]
-
-        at = k if at is None else at
 
         def one(step, carry):
             peer = peer_of(step)
-            pltpu.make_async_remote_copy(
-                cut(source, peer),
-                cut(target, me),
-                send_sems.at[at],
-                recv_sems.at[at],
-                device_id={"lat": peer},
-                device_id_type=MESH,
-            ).start()
+
+            def send_to_peer():
+                for at, part in parts or ((k, None),):
+                    pltpu.make_async_remote_copy(
+                        cut(source, peer, part),
+                        cut(target, me, part),
+                        send_sems.at[at],
+                        recv_sems.at[at],
+                        device_id={"lat": peer},
+                        device_id_type=MESH,
+                    ).start()
+
+            if only is None:
+                send_to_peer()
+            else:
+                pl.when(only(peer))(send_to_peer)
             return carry
 
         lax.fori_loop(*steps, one, 0)
@@ -219,14 +223,20 @@
     pl.semaphore_wait(far_sem, 2)
     exchange(send, recv, send_sem, recv_sem, 0, steps=(1, near_from))
 
-    live = counts[me]
+    def entry(row, at):
+        lane = lax.broadcasted_iota(jnp.int32, row.shape, 1)
+        chosen = jnp.where(lane == at, row.astype(F32), 0.0)
+        return jnp.sum(chosen, axis=1, keepdims=True)
+
+    loads[2].wait()
+    live = entry(count_row[...], me)
     step_rows = 96
 
     def sums(i, carry):
         first, second = carry
         s = i // (padded_points // step_rows)
         r = pl.multiple_of(lax.rem(i, padded_points // step_rows) * step_rows, step_rows)
-        on = jnp.where(s < live, 1.0, 0.0).astype(F32)
+        on = jnp.where(lax.convert_element_type(s, F32) < live, 1.0, 0.0).astype(F32)
         values = x[s, pl.ds(r, step_rows), :].astype(F32) * on
         values = values.reshape(step_rows // 8, 8, values.shape[1])
         return first + jnp.sum(values, axis=0), second + jnp.sum(values * values, axis=0)
@@ -281,7 +291,7 @@
             )
         exchange(send, recv, send_sem, recv_sem, k)
 
-    for load in loads[2:]:
+    for load in loads[3:]:
         load.wait()
     row = lax.broadcasted_iota(jnp.int32, (n * slots, n), 0)
     device = lax.broadcasted_iota(jnp.int32, (n * slots, n), 1)
@@ -342,8 +352,11 @@
         lax.fori_loop(0, n, widen, 0)
 
         def wave(w, inner):
-            number = owner[me * chunks * PAIR + k * PAIR + w]
-            is_zero = jnp.where(number == 0, 1.0, 0.0).astype(F32)
+            wave_slot = me * chunks * PAIR + k * PAIR + w
+            number = jnp.zeros((1, 1), F32)
+            for i in range(number_row.shape[0]):
+                number = number + entry(number_row[i : i + 1, :], wave_slot - i * LANES)
+            is_zero = jnp.where(number == 0.0, 1.0, 0.0).astype(F32)
             for h in range(2):
                 m_h, s_h = mean[h : h + 1], scale[h : h + 1]
                 re = flat[pl.ds(w * 4 + h, rows, stride=ROWS), :]
@@ -360,7 +373,7 @@
                     ).astype(BF16)
             here = padded[k * PAIR + w]
             coefficient = dot(here, weighted[...], (0, 0))
-            keep = lax.broadcasted_iota(jnp.int32, (degrees, 1), 0) >= number
+            keep = lax.broadcasted_iota(jnp.int32, (degrees, 1), 0).astype(F32) >= number
             factor = jnp.where(keep, gain[...], 0.0)
             for t in range(2):
                 cols = slice(2 * t * LANES, 2 * (t + 1) * LANES)
@@ -397,8 +410,13 @@
     lax.fori_loop(0, last, legendre_and_return, 0)
     legendre(last, 0)
     parts = ((0, early), (early, slots - early))
-    for i, part in enumerate(parts):
-        exchange(back_send, back_recv, back_send_sem, back_recv_sem, last, part, last + i)
+    named = [(last + i, part) for i, part in enumerate(parts)]
+    for some, only in (
+        (named, lambda peer: peer < n // 2),
+        (named[:1], lambda peer: peer >= n // 2),
+        (named[1:], lambda peer: peer >= n // 2),
+    ):
+        exchange(back_send, back_recv, back_send_sem, back_recv_sem, last, some, only)
 
     def spread(k, s):
         flat[pl.ds(0, 2 * quads), :] = (
@@ -466,7 +484,6 @@
     quads = n * PAIR * 2
     rows = n * slots
     waves = wave_rows(owner_wavenumber.shape[0], longitudes, padded_half)
-    smem = pl.BlockSpec(memory_space=pltpu.SMEM)
     anywhere = pl.BlockSpec(memory_space=pl.ANY)
     message = (chunks, n, slots, ROWS, LANES)
     dma = pltpu.SemaphoreType.DMA
@@ -475,7 +492,7 @@
     return pl.pallas_call(
         functools.partial(kernel, dims),
         out_shape=pltpu.VMEM(grid_values.shape, BF16),
-        in_specs=[smem, smem] + [anywhere] * 8,
+        in_specs=[anywhere] * 8,
         out_specs=pl.BlockSpec(memory_space=pltpu.VMEM),
         scratch_shapes=[
             pltpu.VMEM((slots, padded_points, channels), BF16),
@@ -522,8 +539,6 @@
             collective_id=0, has_side_effects=True, vmem_limit_bytes=54 * 1024 * 1024
         ),
     )(
-        lat_counts,
-        owner_wavenumber,
         grid_values,
         waves,
         legendre,

time: 510 us -> 509 us (level)
  no operation moved by 1% of the time
where the time goes in v4:
time: 509 us
  Pallas kernels  507 us (100%)
    pallas_call x1, Pallas kernels, body(): pl.pallas_call(functools.partial(kernel, dims), out_shape=pltpu.VMEM(grid...  507 us

profile of v4, /device:TPU:37, one launch (start us, length us, event | category | flops | bytes accessed | tf_op | source)
XLA Modules:
  0.0 509.4 jit_solution(8872423698287435914)
XLA Ops:
  0.0 507.1 %shard_map.82 = bf16[7,1440,256]{2,1,0:T(8,128)(2,1)S(1)} custom-call(bf16[7,1440,256]{2,1,0:T(8,128)(2,1)} %x_hbm.1, bf16[768,896]{1,0:T(8,128)(2,1)} %constant.2.clone.waves_hbm, bf16[6,384,384]{2,1,0:T(8,128)(2,1)} %leg_hbm.1, s32[3,128]{1,0:T(4,128)} %bitcast.3, s32[1,64]{1,0:T(1,128)} %bitcast.5, f32[3,128]{1,0:T(4,128)} %bitcast.4, ...), custom_call_target="tpu_custom_call" | custom-call | tf_op jit(solution)/shard_map/pallas_call | solution.py:492
  507.1 2.3 copy.10

commit v5 on v4

--- a/solution.py
+++ b/solution.py
@@ -411,11 +411,14 @@
     legendre(last, 0)
     parts = ((0, early), (early, slots - early))
     named = [(last + i, part) for i, part in enumerate(parts)]
-    for some, only in (
-        (named, lambda peer: peer < n // 2),
-        (named[:1], lambda peer: peer >= n // 2),
-        (named[1:], lambda peer: peer >= n // 2),
-    ):
+
+    def first_half(peer):
+        return lax.rem(peer + 3 * n // 16, n) < n // 2
+
+    def second_half(peer):
+        return lax.rem(peer + 3 * n // 16, n) >= n // 2
+
+    for some, only in ((named, first_half), (named[:1], second_half), (named[1:], second_half)):
         exchange(back_send, back_recv, back_send_sem, back_recv_sem, last, some, only)
 
     def spread(k, s):

time: 509 us -> 505 us (level)
  Pallas kernels: 507 us -> 500 us
    pallas_call x1, Pallas kernels: 507 us -> 500 us  [body(): pl.pallas_call(functools.partial(kernel, dims), out_shape=pltpu.VMEM(grid...]
where the time goes in v5:
time: 505 us; the launch traced here: 502 us
  Pallas kernels  500 us (99%)
    pallas_call x1, Pallas kernels, body(): pl.pallas_call(functools.partial(kernel, dims), out_shape=pltpu.VMEM(grid...  500 us

profile of v5, /device:TPU:37, one launch (start us, length us, event | category | flops | bytes accessed | tf_op | source)
XLA Modules:
  0.0 502.4 jit_solution(17455894292170554879)
XLA Ops:
  0.0 500.1 %shard_map.82 = bf16[7,1440,256]{2,1,0:T(8,128)(2,1)S(1)} custom-call(bf16[7,1440,256]{2,1,0:T(8,128)(2,1)} %x_hbm.1, bf16[768,896]{1,0:T(8,128)(2,1)} %constant.2.clone.waves_hbm, bf16[6,384,384]{2,1,0:T(8,128)(2,1)} %leg_hbm.1, s32[3,128]{1,0:T(4,128)} %bitcast.3, s32[1,64]{1,0:T(1,128)} %bitcast.5, f32[3,128]{1,0:T(4,128)} %bitcast.4, ...), custom_call_target="tpu_custom_call" | custom-call | tf_op jit(solution)/shard_map/pallas_call | solution.py:495
  500.1 2.3 copy.10
